TPU v7x, 256 devices: a whole 4x4x8 slice. The times are simulated.
256 devices in a mesh: grp: 8 (over x, core), mem: 32 (over z, y).
Axes of the slice: x: 4, y: 4, z: 8, core: 2. Of those that a mesh axis runs over, the one named last changes fastest.
Arguments:
- slab: float32 [2048, 16384], P('mem', 'grp'), may hold values from 0 to 32, as said below
- tiles: float32 [8192, 16384], P('grp', 'mem'), may hold values from 0 to 1.05, as said below
- slot_rows: int32 [16, 32], P('grp'), may hold values from -1 to 3, as said below
Outputs:
- clustered: float32 [2048, 16384], P('grp', 'mem')
Inputs may be any that keep to these rules, and one draw needn't show every extreme that they name: For each group g and block column m, the used slots h (slot_rows[g * 2 + h, m] >= 0) come first and name distinct block rows of the group; unused slots hold -1. Each block column has at least one used slot in every group, and in every draw some group and block column has all 2 slots used. Entries are nonnegative, positive in the tiles of used slots, and zero in the tiles of unused slots. `slab`: entries are positive.
All inputs are finite; a program needn't handle non-finite values.
Results may differ from a plain program's by a relative error of at most 0.0003.
Values sent between devices are 32-bit elements; how exact they have to be, the bound alone decides.
A program may use at most 64 MiB of HBM per device.

v0:
```python
import jax
import jax.numpy as jnp
from jax import lax
from jax.sharding import PartitionSpec as P


def per_device(slab, tiles, slot_rows):
    tile_size = tiles.shape[1]
    slot_total = tiles.shape[0] // tile_size
    member = lax.axis_index("mem")
    own_rows = lax.dynamic_index_in_dim(slot_rows, member, axis=1, keepdims=False)
    used_slots = jnp.sum((own_rows >= 0).astype(jnp.int32))
    block_rows = jnp.maximum(own_rows, 0)
    tile_stack = tiles.reshape(slot_total, tile_size, tile_size)
    row_piece = lax.all_gather(slab, "mem", axis=0, tiled=True)

    def add_slot(slot_index, running):
        columns = lax.dynamic_slice_in_dim(
            row_piece, block_rows[slot_index] * tile_size, tile_size, 1
        )
        return running + jnp.dot(
            columns,
            tile_stack[slot_index],
            preferred_element_type=jnp.float32,
            precision=lax.Precision.HIGHEST,
        )

    partial_sums = lax.fori_loop(
        0, used_slots, add_slot, jnp.zeros((row_piece.shape[0], tile_size), jnp.float32)
    )
    window_rows = partial_sums.shape[0]
    expanded = lax.psum_scatter(partial_sums, "grp", scatter_dimension=0, tiled=True)
    inflated = expanded * expanded
    column_sums = lax.psum(jnp.sum(inflated, axis=0), "grp")
    column_means = column_sums / window_rows
    return inflated / column_means


def solution(mesh):
    return jax.shard_map(
        per_device,
        mesh=mesh,
        in_specs=(P("mem", "grp"), P("grp", "mem"), P("grp", None)),
        out_specs=P("grp", "mem"),
        check_vma=False,
    )
```

profile of v0, /device:TPU:1, one launch (start us, length us, event | category | flops | bytes accessed | tf_op | source)
XLA Modules:
  0.0 241.1 jit_solution(9636385513887879012)
XLA Ops:
  6.5 0.0 copy-start
  6.5 0.0 all-gather.2.cloned.1.call-start
  6.5 0.7 all-gather.2.cloned.1.call-update
  7.3 0.0 reduce-scatter.2.cloned.1.call-start
  7.3 1.4 maximum_reduce_fusion
  8.8 143.9 %all-gather.2.cloned.1.call-done = f32[2048,2048]{1,0:T(8,128)} async-done(((f32[64,2048]{1,0:T(8,128)}), f32[2048,2048]{1,0:T(8,128)}) %all-gather.2.cloned.1.call-update) | async-done | bytes 16777232 | tf_op jit(solution)/shard_map/all_gather | solution.py:15
  152.7 2.5 %broadcast_in_dim.4 = f32[2048,512]{1,0:T(8,128)} broadcast(f32[]{:T(128)} %constant.7.clone.1), dimensions={} | broadcast | bytes 4194308 | tf_op jit(solution)/shard_map/broadcast_in_dim | solution.py:29
  155.2 0.0 copy-done
  155.2 12.9 %while.10 = (s32[]{:T(128)}, f32[2048,512]{1,0:T(8,128)}, s32[]{:T(128)}, s32[2]{0:T(128)S(1)}, f32[2048,2048]{1,0:T(8,128)}, /*index=5*/f32[2,512,512]{2,1,0:T(...) while((s32[]{:T(128)}, f32[2048,512]{1,0:T(8,128)}, s32[]{:T(128)}, ...), condition=%wide.region_2.3_spmd, body=%wide.region_1.2_spmd.sunk | while | flops 6443499520 | bytes 13631705 | solution.py:28
  155.8 0.6 dynamic_slice.29
  157.0 10.4 %fusion.14 = f32[2048,512]{1,0:T(8,128)} fusion(f32[2048,512]{1,0:T(8,128)} %get-tuple-element.103, f32[2048,2048]{1,0:T(8,128)} %get-tuple-element.117, s32[]{:T(128)S(6)} %select_n.15, f32[2,512,512]{2,1,0:T(8,128)S(1)} %get-tuple-element.118, s32[]{:T(128)S(6)} %select_n.14), kind=kOutput, calls=%fused_computation.2.clone.1 | convolution fusion | flops 6443499520 | bytes 13631496 | tf_op jit(solution)/shard_map/while/body/dot_general | solution.py:21
  168.1 0.0 reduce-scatter.2.cloned.1.call-update
  168.1 48.0 %reduce-scatter.2.cloned.1.call-done = f32[256,512]{1,0:T(8,128)} async-done(((f32[2048,512]{1,0:T(8,128)}), f32[256,512]{1,0:T(8,128)}) %reduce-scatter.2.cloned.1.call-update) | async-done | bytes 524304 | tf_op jit(solution)/shard_map/reduce_scatter | solution.py:32
  216.1 1.1 multiply_reduce_fusion
  217.2 15.2 %psum.7 = f32[512]{0:T(512)S(1)} all-reduce(f32[512]{0:T(512)S(1)} %multiply_reduce_fusion), channel_id=1, replica_groups=mesh['grp'=8,'mem'=32] {'grp'}, use_global_device_ids=true, to_apply=%region_5.6 | all-reduce | flops 512 | bytes 4096 | tf_op jit(solution)/shard_map/psum | solution.py:34
  232.4 1.9 multiply_divide_fusion
  (1 shorter events, 0.0 us)
Async XLA Ops:
  6.5 148.6 %copy-start = (f32[1024,512]{1,0:T(8,128)S(1)}, f32[1024,512]{1,0:T(8,128)}, u32[]{:S(2)}) copy-start(f32[1024,512]{1,0:T(8,128)} %param.6) | copy-start | bytes 6291460
  6.5 146.2 %all-gather.2.cloned.1.call-start = ((), (), s32[]{:S(2)}) async-start(), calls=%async_computation.1 | async-start | bytes 17301504 | tf_op jit(solution)/shard_map/all_gather | solution.py:15
  7.3 208.8 %reduce-scatter.2.cloned.1.call-start = ((), (), s32[]{:S(2)}) async-start(), calls=%async_computation.2 | async-start | bytes 4718592 | tf_op jit(solution)/shard_map/reduce_scatter | solution.py:32
Sparse Core Ops, SparseCore 0:
  9.9 142.7 all-gather.1
  168.2 47.8 reduce-scatter.1
where the time goes:
time: 241 us
  waiting for transfers between devices  193 us (80%)
  blocking collectives  15.2 us (6%)
  between operations  13.4 us (6%)
  matrix products  10.4 us (4%)
  other arithmetic  4.47 us (2%)
  local copies, waits for them, and re-layouts  3.05 us (1%)
    all_gather x1, waiting for transfers between devices, per_device(): row_piece = lax.all_gather(slab, 'mem', axis=0, tiled=True)  144 us
    reduce_scatter x1, waiting for transfers between devices, per_device(): lax.psum_scatter(partial_sums, 'grp', scatter_dimension=0, tiled=True)  48 us
    psum x1, blocking collectives, per_device(): column_sums = lax.psum(jnp.sum(inflated, axis=0), 'grp')  15.2 us
    dot_general x1, matrix products, add_slot(): jnp.dot(columns, tile_stack[slot_index], preferred_element_type=jnp.float...  10.4 us
  transfers between devices with their start and end apart: 2, of which 2 were waited for; matrix products, arithmetic and copies ran while one was open for 1% of the time, Pallas kernels for 0%

commit v1 on v0

v1 whole, which is shorter than its diff:
```python
import functools

import jax
import jax.numpy as jnp
from jax import lax
from jax.experimental import pallas as pl
from jax.experimental.pallas import tpu as pltpu
from jax.sharding import PartitionSpec as P

MESH = pl.DeviceIdType.MESH
F32 = jnp.float32
BF16 = jnp.bfloat16

TILE = 512
ROWS = 64
KCOLS = 2048
HALF = 1024
ZN, YN, XN, GN = 8, 4, 4, 8
WROWS = 2048

UP, DOWN, ACROSS = 0, 1, 2
NA, NB = 0, 1
LO, HI = 0, 1


def body(
    slab, tiles, slot_rows, out,
    rows, tile_buf, thi, tlo, xhi, xlo, part, sib, csum, mid, dst, ybuf, fin, stage, sq, sq_all,
    load_sem, gsend, grecv, tsend, trecv, dsend, drecv, xsend, mrecv, rrecv, ysend, yrecv, qsend, qrecv,
):
    g = lax.axis_index("grp")
    m = lax.axis_index("mem")
    x, core = g // 2, g % 2
    z, y = m // YN, m % YN
    pair_y = y + 1 - 2 * (y % 2)
    m_up = ((z + 1) % ZN) * YN + y
    m_down = ((z + ZN - 1) % ZN) * YN + y
    m_across = z * YN + (3 - y)
    m_pair = z * YN + pair_y
    g_sib = x * 2 + (1 - core)

    def dev(gi, mi):
        return {"grp": gi, "mem": mi}

    load_slab = pltpu.make_async_copy(slab, rows.at[NA, 0], load_sem.at[0])
    load_tiles = pltpu.make_async_copy(tiles, tile_buf.at[0], load_sem.at[1])
    load_slab.start()
    load_tiles.start()

    barrier = pltpu.get_barrier_semaphore()
    for mi in (m_up, m_down, m_across, m_pair):
        pl.semaphore_signal(barrier, inc=1, device_id=dev(g, mi), device_id_type=MESH)
    for d in range(1, GN):
        pl.semaphore_signal(barrier, inc=1, device_id=dev((g + d) % GN, m), device_id_type=MESH)
    pl.semaphore_wait(barrier, 4 + GN - 1)

    started = []

    def piece(w, s, h):
        return rows.at[w, s, :, pl.ds(h * HALF, HALF)]

    def move(way, w, s, h):
        if way == ACROSS:
            target, tw, ts = m_across, NB, s
        elif way == UP:
            target, tw, ts = m_up, w, s + 1
        else:
            target, tw, ts = m_down, w, (s + 7) % 8
        copy = pltpu.make_async_remote_copy(
            src_ref=piece(w, s, h), dst_ref=piece(tw, ts, h),
            send_sem=gsend.at[len(started)], recv_sem=grecv.at[tw, ts, h],
            device_id=dev(g, target), device_id_type=MESH,
        )
        copy.start()
        started.append(copy)

    def split(w, s, h):
        for b in range(2):
            block = s * 4 + h * 2 + b
            v = rows[w, s, :, pl.ds(h * HALF + b * TILE, TILE)]
            top = v.astype(BF16)
            xhi[block, pl.ds(w * ROWS, ROWS), :] = top
            xlo[block, pl.ds(w * ROWS, ROWS), :] = (v - top.astype(F32)).astype(BF16)

    def arrive(w, s, h):
        pltpu.make_async_remote_copy(
            src_ref=piece(w, s, h), dst_ref=piece(w, s, h),
            send_sem=gsend.at[0], recv_sem=grecv.at[w, s, h],
            device_id=dev(g, m_up), device_id_type=MESH,
        ).wait_recv()

    tile_copies = [
        pltpu.make_async_remote_copy(
            src_ref=tile_buf.at[0, pl.ds(h * TILE, TILE)], dst_ref=tile_buf.at[1, pl.ds(h * TILE, TILE)],
            send_sem=tsend.at[h], recv_sem=trecv.at[h],
            device_id=dev(g, m_pair), device_id_type=MESH,
        )
        for h in range(2)
    ]

    def split_tile(p, h):
        def step(i, carry):
            r = pl.multiple_of(i * 64, 64)
            v = tile_buf[p, pl.ds(h * TILE + r, 64), :]
            top = v.astype(BF16)
            thi[p * 2 + h, pl.ds(r, 64), :] = top
            tlo[p * 2 + h, pl.ds(r, 64), :] = (v - top.astype(F32)).astype(BF16)
            return carry
        lax.fori_loop(0, TILE // 64, step, 0)

    def product(s, p):
        member = m if p == 0 else m_pair
        u = s * 2 + p
        total = None
        for h in range(2):
            block = s * 4 + jnp.maximum(slot_rows[h, member], 0)
            a, b = xhi[block], xlo[block]
            c, d = thi[p * 2 + h], tlo[p * 2 + h]
            term = (
                jnp.dot(a, d, preferred_element_type=F32)
                + jnp.dot(b, c, preferred_element_type=F32)
                + jnp.dot(a, c, preferred_element_type=F32)
            )
            total = term if total is None else total + term
        part[u] = total.reshape(2, ROWS, TILE)
        sibling(u).start()

    def sibling(u):
        return pltpu.make_async_remote_copy(
            src_ref=part.at[u, 1 - core], dst_ref=sib.at[u],
            send_sem=dsend.at[u], recv_sem=drecv.at[u],
            device_id=dev(g_sib, m), device_id_type=MESH,
        )

    def place(s):
        zt = (z - s + ZN) % ZN
        xt, ct = zt // 2, zt % 2
        return xt, ct, (xt - x + XN) % XN

    def to_mid(u):
        xm = (x + 1 + 2 * core) % XN
        return pltpu.make_async_remote_copy(
            src_ref=csum.at[u], dst_ref=mid.at[u],
            send_sem=xsend.at[u], recv_sem=mrecv.at[u],
            device_id=dev(xm * 2 + core, m), device_id_type=MESH,
        )

    def to_dst(u, s, p):
        xt, ct, dx = place(s)
        side = jnp.where(dx == 1, 0, jnp.where(dx == 0, 1, 2))
        slot = p * 6 + side * 2 + core
        return pltpu.make_async_remote_copy(
            src_ref=csum.at[u], dst_ref=dst.at[slot],
            send_sem=xsend.at[u], recv_sem=rrecv.at[slot],
            device_id=dev(xt * 2 + ct, m), device_id_type=MESH,
        )

    def is_mid(dx):
        return ((dx == 1) & (core == 0)) | ((dx == 3) & (core == 1))

    def chip_sum(s, p):
        u = s * 2 + p
        xt, ct, dx = place(s)
        sibling(u).wait_recv()
        csum[u] = part[u, core] + sib[u]

        @pl.when(dx == 2)
        def _():
            to_mid(u).start()

        @pl.when(((dx == 0) & (ct != core)) | ((dx == 1) & (core == 1)) | ((dx == 3) & (core == 0)))
        def _():
            to_dst(u, s, p).start()

    def middle_sum(s, p):
        u = s * 2 + p
        xt, ct, dx = place(s)

        @pl.when(is_mid(dx))
        def _():
            to_mid(u).wait_recv()
            csum[u] = csum[u] + mid[u]
            to_dst(u, s, p).start()

    def finish(units):
        for s, p in units:
            chip_sum(s, p)
        for s, p in units:
            middle_sum(s, p)

    load_slab.wait()
    for h in (LO, HI):
        move(UP, NA, 0, h)
        move(DOWN, NA, 0, h)
        move(ACROSS, NA, 0, h)
    load_tiles.wait()
    for copy in tile_copies:
        copy.start()
    for h in (LO, HI):
        split(NA, 0, h)
    for h in range(2):
        split_tile(0, h)

    def arrive_near(h, s_up, s_down):
        arrive(NA, s_up, h)
        move(UP, NA, s_up, h)
        arrive(NA, s_down, h)
        move(DOWN, NA, s_down, h)

    for h in (LO, HI):
        arrive_near(h, 1, 7)
        move(ACROSS, NA, 1, h)
        move(ACROSS, NA, 7, h)
        split(NA, 1, h)
        split(NA, 7, h)
        arrive(NB, 0, h)
        split(NB, 0, h)
    product(0, 0)
    arrive_near(LO, 2, 6)
    arrive(NB, 1, LO)
    move(UP, NB, 1, LO)
    split(NA, 2, LO)
    split(NA, 6, LO)
    split(NB, 1, LO)
    arrive_near(HI, 2, 6)
    move(ACROSS, NA, 2, HI)
    arrive(NB, 7, LO)
    move(DOWN, NB, 7, LO)
    split(NA, 2, HI)
    split(NA, 6, HI)
    split(NB, 7, LO)
    finish([(0, 0)])
    arrive(NA, 3, LO)
    arrive(NA, 5, LO)
    split(NA, 3, LO)
    split(NA, 5, LO)
    arrive(NB, 1, HI)
    split(NB, 1, HI)
    product(1, 0)
    arrive(NB, 2, LO)
    move(UP, NB, 2, LO)
    move(UP, NA, 3, LO)
    arrive(NB, 6, LO)
    move(DOWN, NB, 6, LO)
    split(NB, 2, LO)
    split(NB, 6, LO)
    arrive(NB, 7, HI)
    split(NB, 7, HI)
    product(7, 0)
    finish([(1, 0)])
    arrive(NA, 3, HI)
    arrive(NA, 5, HI)
    move(ACROSS, NA, 5, HI)
    move(DOWN, NA, 5, HI)
    move(ACROSS, NA, 3, HI)
    move(ACROSS, NA, 6, HI)
    split(NA, 3, HI)
    split(NA, 5, HI)
    arrive(NB, 2, HI)
    split(NB, 2, HI)
    product(2, 0)
    finish([(7, 0)])
    arrive(NB, 3, LO)
    move(UP, NB, 3, LO)
    arrive(NB, 5, LO)
    split(NB, 3, LO)
    split(NB, 5, LO)
    arrive(NB, 5, HI)
    move(DOWN, NB, 5, HI)
    split(NB, 5, HI)
    product(5, 0)
    finish([(2, 0)])
    for h in range(2):
        tile_copies[h].wait_recv()
        split_tile(1, h)
    for s in (0, 1, 7):
        product(s, 1)
    finish([(5, 0), (0, 1), (1, 1), (7, 1)])
    for s in (2, 5):
        product(s, 1)
    arrive(NA, 4, LO)
    arrive(NA, 4, HI)
    split(NA, 4, LO)
    split(NA, 4, HI)
    arrive(NB, 3, HI)
    split(NB, 3, HI)
    product(3, 0)
    product(3, 1)
    finish([(2, 1), (5, 1), (3, 0), (3, 1)])
    for h in (LO, HI):
        arrive(NB, 4, h)
        split(NB, 4, h)
    product(4, 0)
    product(4, 1)
    arrive(NB, 6, HI)
    split(NB, 6, HI)
    product(6, 0)
    product(6, 1)
    finish([(4, 0), (4, 1), (6, 0), (6, 1)])

    s_mine = (z - g + ZN) % ZN

    def received(p, side, w):
        slot = p * 6 + side * 2 + w
        pltpu.make_async_remote_copy(
            src_ref=csum.at[0], dst_ref=dst.at[slot],
            send_sem=xsend.at[0], recv_sem=rrecv.at[slot],
            device_id=dev(g_sib, m), device_id_type=MESH,
        ).wait_recv()

    def sums(p):
        own = s_mine * 2 + p
        for side in (0, 2):
            for w in range(2):
                received(p, side, w)
        received(p, 1, 1 - core)
        other = 1 - core
        return (
            dst[p * 6 + core] + dst[p * 6 + 4 + core] + csum[own],
            dst[p * 6 + other] + dst[p * 6 + 4 + other] + dst[p * 6 + 2 + other],
        )

    across, behind = sums(1)
    ybuf[core] = across
    ybuf[1 - core] = behind
    to_pair = pltpu.make_async_remote_copy(
        src_ref=ybuf, dst_ref=fin, send_sem=ysend, recv_sem=yrecv,
        device_id=dev(g, m_pair), device_id_type=MESH,
    )
    to_pair.start()

    def keep(row_y, v):
        v = v * v
        stage[row_y] = v
        return jnp.sum(v.reshape(ROWS // 8, 8, TILE), axis=0)

    turn = 3 - 2 * y
    mine, theirs = sums(0)
    total = keep(y + core * turn, mine) + keep(y + (1 - core) * turn, theirs)
    to_pair.wait()
    total += keep(pair_y, fin[0]) + keep(3 - pair_y, fin[1])
    sq[...] = total

    def square_copy(d):
        return pltpu.make_async_remote_copy(
            src_ref=sq, dst_ref=sq_all.at[d - 1], send_sem=qsend.at[d - 1], recv_sem=qrecv.at[d - 1],
            device_id=dev((g + d) % GN, m), device_id_type=MESH,
        )

    for d in range(1, GN):
        square_copy(d).start()
    for d in range(1, GN):
        square_copy(d).wait_recv()
        total += sq_all[d - 1]
    means = jnp.sum(total, axis=0, keepdims=True) / WROWS
    for row_y in range(YN):
        out[pl.ds(row_y * ROWS, ROWS), :] = stage[row_y] / means

    for copy in started:
        copy.wait_send()
    for copy in tile_copies:
        copy.wait_send()
    for s in range(8):
        xt, ct, dx = place(s)
        for p in range(2):
            sibling(s * 2 + p).wait_send()

            @pl.when((dx != 0) | (ct != core))
            def _():
                to_mid(s * 2 + p).wait_send()

    for d in range(1, GN):
        square_copy(d).wait_send()


def per_device(slab, tiles, slot_rows):
    dma = pltpu.SemaphoreType.DMA
    return pl.pallas_call(
        body,
        out_shape=jax.ShapeDtypeStruct((256, TILE), F32),
        in_specs=[
            pl.BlockSpec(memory_space=pltpu.HBM),
            pl.BlockSpec(memory_space=pltpu.HBM),
            pl.BlockSpec(memory_space=pltpu.SMEM),
        ],
        out_specs=pl.BlockSpec(memory_space=pltpu.VMEM),
        scratch_shapes=[
            pltpu.VMEM((2, 8, ROWS, KCOLS), F32),
            pltpu.VMEM((2, 2 * TILE, TILE), F32),
            pltpu.VMEM((4, TILE, TILE), BF16),
            pltpu.VMEM((4, TILE, TILE), BF16),
            pltpu.VMEM((32, 2 * ROWS, TILE), BF16),
            pltpu.VMEM((32, 2 * ROWS, TILE), BF16),
            pltpu.VMEM((16, 2, ROWS, TILE), F32),
            pltpu.VMEM((16, ROWS, TILE), F32),
            pltpu.VMEM((16, ROWS, TILE), F32),
            pltpu.VMEM((16, ROWS, TILE), F32),
            pltpu.VMEM((12, ROWS, TILE), F32),
            pltpu.VMEM((2, ROWS, TILE), F32),
            pltpu.VMEM((2, ROWS, TILE), F32),
            pltpu.VMEM((4, ROWS, TILE), F32),
            pltpu.VMEM((8, TILE), F32),
            pltpu.VMEM((GN - 1, 8, TILE), F32),
            dma((2,)),
            dma((32,)),
            dma((2, 8, 2)),
            dma((2,)),
            dma((2,)),
            dma((16,)),
            dma((16,)),
            dma((16,)),
            dma((16,)),
            dma((12,)),
            dma,
            dma,
            dma((GN - 1,)),
            dma((GN - 1,)),
        ],
        compiler_params=pltpu.CompilerParams(
            collective_id=0, has_side_effects=True, vmem_limit_bytes=60 * 1024 * 1024
        ),
        name="expand",
    )(slab, tiles, slot_rows)


def solution(mesh):
    return jax.shard_map(
        per_device,
        mesh=mesh,
        in_specs=(P("mem", "grp"), P("grp", "mem"), P("grp", None)),
        out_specs=P("grp", "mem"),
        check_vma=False,
    )
```

time: 241 us -> 111 us (0.46)
  waiting for transfers between devices: 193 us -> 0 us
  Pallas kernels: 0 us -> 109 us
  blocking collectives: 15.2 us -> 0 us
  between operations: 13.4 us -> 0.01 us
  matrix products: 10.4 us -> 0 us
  other arithmetic: 4.47 us -> 0 us
    all_gather x1 -> x0, waiting for transfers between devices: 144 us -> none  [per_device(): row_piece = lax.all_gather(slab, 'mem', axis=0, tiled=True)]
    pallas_call x0 -> x1, Pallas kernels: none -> 109 us  [per_device(): pl.pallas_call(body, out_shape=jax.ShapeDtypeStruct((256, TILE), F32), in...]
    reduce_scatter x1 -> x0, waiting for transfers between devices: 48 us -> none  [per_device(): lax.psum_scatter(partial_sums, 'grp', scatter_dimension=0, tiled=True)]
    psum x1 -> x0, blocking collectives: 15.2 us -> none  [per_device(): column_sums = lax.psum(jnp.sum(inflated, axis=0), 'grp')]
    dot_general x1 -> x0, matrix products: 10.4 us -> none  [add_slot(): jnp.dot(columns, tile_stack[slot_index], preferred_element_type=jnp.float...]
    broadcast_in_dim x1 -> x0, local copies, waits for them, and re-layouts: 2.46 us -> none  [per_device(): jnp.zeros((row_piece.shape[0], tile_size), jnp.float32)]
  transfers between devices with their start and end apart: 2 -> 0, of which waited for: 2 -> 0; matrix products, arithmetic and copies ran while one was open for 1% -> 0% of each run, Pallas kernels for 0% -> 0%
where the time goes in v1:
time: 111 us
  Pallas kernels  109 us (98%)
  local copies, waits for them, and re-layouts  1.87 us (2%)
    pallas_call x1, Pallas kernels, per_device(): pl.pallas_call(body, out_shape=jax.ShapeDtypeStruct((256, TILE), F32), in...  109 us

profile of v1, /device:TPU:1, one launch (start us, length us, event | category | flops | bytes accessed | tf_op | source)
XLA Modules:
  0.0 110.7 jit_solution(1240295300817352081)
XLA Ops:
  0.0 108.9 %expand.1 = f32[256,512]{1,0:T(8,128)} custom-call(f32[64,2048]{1,0:T(8,128)} %slab.1, f32[1024,512]{1,0:T(8,128)} %tiles.1, s32[2,32]{1,0:T(2,128)} %slot_rows.1), custom_call_target="tpu_custom_call" | custom-call | tf_op jit(solution)/shard_map/expand/pallas_call | solution.py:378
  108.9 1.9 %copy.5 = f32[256,512]{1,0:T(8,128)} copy(f32[256,512]{1,0:T(8,128)} %expand.1) | data formatting | bytes 1048576

commit v2 on v1

v2 whole, which is shorter than its diff:
```python
import functools

import jax
import jax.numpy as jnp
from jax import lax
from jax.experimental import pallas as pl
from jax.experimental.pallas import tpu as pltpu
from jax.sharding import PartitionSpec as P

MESH = pl.DeviceIdType.MESH
F32 = jnp.float32
BF16 = jnp.bfloat16

TILE = 512
ROWS = 64
KCOLS = 2048
HALF = 1024
WIDTH = 256
ZN, YN, XN, GN = 8, 4, 4, 8
WROWS = 2048

UP, DOWN, ACROSS = 0, 1, 2
NA, NB = 0, 1
LO, HI = 0, 1


def body(
    slab, tiles, slot_rows, out,
    rows, tile_buf, thi, tlo, xhi, xlo, part, sib, csum, mid, dst, near, ybuf, fin, stage, sq, sq_all,
    load_sem, gsend, grecv, tsend, trecv, dsend, drecv, xsend, mrecv, rrecv, nrecv, ysend, yrecv, qsend, qrecv,
):
    g = lax.axis_index("grp")
    m = lax.axis_index("mem")
    x, core = g // 2, g % 2
    z, y = m // YN, m % YN
    pair_y = y + 1 - 2 * (y % 2)
    m_up = ((z + 1) % ZN) * YN + y
    m_down = ((z + ZN - 1) % ZN) * YN + y
    m_across = z * YN + (3 - y)
    m_pair = z * YN + pair_y
    g_sib = x * 2 + (1 - core)

    def dev(gi, mi):
        return {"grp": gi, "mem": mi}

    load_slab = pltpu.make_async_copy(slab, rows.at[NA, 0], load_sem.at[0])
    load_tiles = pltpu.make_async_copy(tiles, tile_buf.at[0], load_sem.at[1])
    load_slab.start()
    load_tiles.start()

    barrier = pltpu.get_barrier_semaphore()
    for mi in (m_up, m_down, m_across, m_pair):
        pl.semaphore_signal(barrier, inc=1, device_id=dev(g, mi), device_id_type=MESH)
    for d in range(1, GN):
        pl.semaphore_signal(barrier, inc=1, device_id=dev((g + d) % GN, m), device_id_type=MESH)
    pl.semaphore_wait(barrier, 4 + GN - 1)

    started = []

    def piece(w, s, h):
        return rows.at[w, s, :, pl.ds(h * HALF, HALF)]

    def move(way, w, s, h):
        if way == ACROSS:
            target, tw, ts = m_across, NB, s
        elif way == UP:
            target, tw, ts = m_up, w, s + 1
        else:
            target, tw, ts = m_down, w, (s + 7) % 8
        copy = pltpu.make_async_remote_copy(
            src_ref=piece(w, s, h), dst_ref=piece(tw, ts, h),
            send_sem=gsend.at[len(started)], recv_sem=grecv.at[tw, ts, h],
            device_id=dev(g, target), device_id_type=MESH,
        )
        copy.start()
        started.append(copy)

    def split(w, s, h):
        for b in range(2):
            block = s * 4 + h * 2 + b
            v = rows[w, s, :, pl.ds(h * HALF + b * TILE, TILE)]
            top = v.astype(BF16)
            xhi[block, pl.ds(w * ROWS, ROWS), :] = top
            xlo[block, pl.ds(w * ROWS, ROWS), :] = (v - top.astype(F32)).astype(BF16)

    def arrive(w, s, h):
        pltpu.make_async_remote_copy(
            src_ref=piece(w, s, h), dst_ref=piece(w, s, h),
            send_sem=gsend.at[0], recv_sem=grecv.at[w, s, h],
            device_id=dev(g, m_up), device_id_type=MESH,
        ).wait_recv()

    tile_copies = [
        pltpu.make_async_remote_copy(
            src_ref=tile_buf.at[0, :, pl.ds(q * WIDTH, WIDTH)], dst_ref=tile_buf.at[1, :, pl.ds(q * WIDTH, WIDTH)],
            send_sem=tsend.at[q], recv_sem=trecv.at[q],
            device_id=dev(g, m_pair), device_id_type=MESH,
        )
        for q in range(2)
    ]

    def split_tile(c):
        p, q = c // 2, c % 2
        for h in range(2):
            def step(i, carry):
                r = pl.multiple_of(i * 64, 64)
                v = tile_buf[p, pl.ds(h * TILE + r, 64), pl.ds(q * WIDTH, WIDTH)]
                top = v.astype(BF16)
                thi[c * 2 + h, pl.ds(r, 64), :] = top
                tlo[c * 2 + h, pl.ds(r, 64), :] = (v - top.astype(F32)).astype(BF16)
                return carry
            lax.fori_loop(0, TILE // 64, step, 0)

    def product(s, columns):
        for c in columns:
            member = m if c < 2 else m_pair
            u = s * 4 + c
            total = None
            for h in range(2):
                block = s * 4 + jnp.maximum(slot_rows[h, member], 0)
                a, b = xhi[block], xlo[block]
                top, low = thi[c * 2 + h], tlo[c * 2 + h]
                term = (
                    jnp.dot(a, low, preferred_element_type=F32)
                    + jnp.dot(b, top, preferred_element_type=F32)
                    + jnp.dot(a, top, preferred_element_type=F32)
                )
                total = term if total is None else total + term
            part[u] = total.reshape(2, ROWS, WIDTH)
            sibling(u).start()

    def sibling(u):
        return pltpu.make_async_remote_copy(
            src_ref=part.at[u, 1 - core], dst_ref=sib.at[u],
            send_sem=dsend.at[u], recv_sem=drecv.at[u],
            device_id=dev(g_sib, m), device_id_type=MESH,
        )

    def place(s):
        zt = (z - s + ZN) % ZN
        xt, ct = zt // 2, zt % 2
        dx = (xt - x + XN) % XN
        hop = jnp.where(core == 0, 3 - dx, (dx + 3) % 4)
        return xt, ct, hop

    x_next = (x + 1 + 2 * core) % XN

    def to_next(u):
        return pltpu.make_async_remote_copy(
            src_ref=csum.at[u], dst_ref=mid.at[u],
            send_sem=xsend.at[u], recv_sem=mrecv.at[u],
            device_id=dev(x_next * 2 + core, m), device_id_type=MESH,
        )

    def to_end(u, c, ct):
        return pltpu.make_async_remote_copy(
            src_ref=csum.at[u], dst_ref=dst.at[c, core],
            send_sem=xsend.at[u], recv_sem=rrecv.at[c, core],
            device_id=dev(x_next * 2 + ct, m), device_id_type=MESH,
        )

    def to_sibling(u, c):
        return pltpu.make_async_remote_copy(
            src_ref=csum.at[u], dst_ref=near.at[c],
            send_sem=xsend.at[u], recv_sem=nrecv.at[c],
            device_id=dev(g_sib, m), device_id_type=MESH,
        )

    def chip_sum(s, columns):
        xt, ct, hop = place(s)
        for c in columns:
            u = s * 4 + c
            sibling(u).wait_recv()
            csum[u] = part[u, core] + sib[u]

            @pl.when(hop == 0)
            def _():
                to_next(u).start()

            @pl.when((hop == 3) & (ct != core))
            def _():
                to_sibling(u, c).start()

    def chain(s, columns):
        xt, ct, hop = place(s)

        @pl.when((hop == 1) | (hop == 2))
        def _():
            for c in columns:
                u = s * 4 + c
                to_next(u).wait_recv()
                csum[u] = csum[u] + mid[u]

                @pl.when(hop == 1)
                def _():
                    to_next(u).start()

                @pl.when(hop == 2)
                def _():
                    to_end(u, c, ct).start()

    load_slab.wait()
    for h in (LO, HI):
        move(UP, NA, 0, h)
        move(DOWN, NA, 0, h)
        move(ACROSS, NA, 0, h)
    load_tiles.wait()
    for copy in tile_copies:
        copy.start()
    for h in (LO, HI):
        split(NA, 0, h)
    for c in range(2):
        split_tile(c)

    def arrive_near(h, s_up, s_down):
        arrive(NA, s_up, h)
        move(UP, NA, s_up, h)
        arrive(NA, s_down, h)
        move(DOWN, NA, s_down, h)

    first, third, every = (0, 1), (0, 1, 2), (2, 3, 0, 1)
    for h in (LO, HI):
        arrive_near(h, 1, 7)
        move(ACROSS, NA, 1, h)
        move(ACROSS, NA, 7, h)
        split(NA, 1, h)
        split(NA, 7, h)
        arrive(NB, 0, h)
        split(NB, 0, h)
    product(0, first)
    arrive_near(LO, 2, 6)
    arrive(NB, 1, LO)
    move(UP, NB, 1, LO)
    split(NA, 2, LO)
    split(NA, 6, LO)
    split(NB, 1, LO)
    chip_sum(0, first)
    arrive_near(HI, 2, 6)
    move(ACROSS, NA, 2, HI)
    arrive(NB, 7, LO)
    move(DOWN, NB, 7, LO)
    split(NA, 2, HI)
    split(NA, 6, HI)
    split(NB, 7, LO)
    chain(0, first)
    tile_copies[0].wait_recv()
    split_tile(2)
    product(0, (2,))
    arrive(NA, 3, LO)
    arrive(NA, 5, LO)
    split(NA, 3, LO)
    split(NA, 5, LO)
    arrive(NB, 1, HI)
    split(NB, 1, HI)
    product(1, third)
    chip_sum(0, (2,))
    arrive(NB, 2, LO)
    move(UP, NB, 2, LO)
    move(UP, NA, 3, LO)
    arrive(NB, 6, LO)
    move(DOWN, NB, 6, LO)
    split(NB, 2, LO)
    split(NB, 6, LO)
    arrive(NB, 7, HI)
    split(NB, 7, HI)
    product(7, third)
    chip_sum(1, third)
    chain(0, (2,))
    arrive(NA, 3, HI)
    arrive(NA, 5, HI)
    move(ACROSS, NA, 5, HI)
    move(DOWN, NA, 5, HI)
    move(ACROSS, NA, 3, HI)
    move(ACROSS, NA, 6, HI)
    split(NA, 3, HI)
    split(NA, 5, HI)
    arrive(NB, 2, HI)
    split(NB, 2, HI)
    product(2, third)
    chip_sum(7, third)
    chain(1, third)
    arrive(NB, 3, LO)
    move(UP, NB, 3, LO)
    arrive(NB, 5, LO)
    split(NB, 3, LO)
    split(NB, 5, LO)
    tile_copies[1].wait_recv()
    split_tile(3)
    arrive(NB, 5, HI)
    move(DOWN, NB, 5, HI)
    split(NB, 5, HI)
    for s in (0, 1, 7, 2):
        product(s, (3,))
    chip_sum(2, third)
    chain(7, third)
    product(5, every)
    for s in (0, 1, 7, 2):
        chip_sum(s, (3,))
    chain(2, third)
    arrive(NA, 4, LO)
    arrive(NA, 4, HI)
    split(NA, 4, LO)
    split(NA, 4, HI)
    arrive(NB, 3, HI)
    split(NB, 3, HI)
    product(3, every)
    chip_sum(5, every)
    for s in (0, 1, 7, 2):
        chain(s, (3,))
    chip_sum(3, every)
    for h in (LO, HI):
        arrive(NB, 4, h)
        split(NB, 4, h)
    product(4, every)
    chain(5, every)
    arrive(NB, 6, HI)
    split(NB, 6, HI)
    product(6, every)
    chip_sum(4, every)
    chip_sum(6, every)
    chain(3, every)
    chain(4, every)
    chain(6, every)

    s_mine = (z - g + ZN) % ZN

    def received(src, sem):
        pltpu.make_async_remote_copy(
            src_ref=csum.at[0], dst_ref=src, send_sem=xsend.at[0], recv_sem=sem,
            device_id=dev(g_sib, m), device_id_type=MESH,
        ).wait_recv()

    def sums(c):
        for w in range(2):
            received(dst.at[c, w], rrecv.at[c, w])
        received(near.at[c], nrecv.at[c])
        return dst[c, core] + csum[s_mine * 4 + c], dst[c, 1 - core] + near[c]

    to_pair = []
    for q in range(2):
        mine, other = sums(2 + q)
        ybuf[q, core] = mine
        ybuf[q, 1 - core] = other
        copy = pltpu.make_async_remote_copy(
            src_ref=ybuf.at[q], dst_ref=fin.at[q], send_sem=ysend.at[q], recv_sem=yrecv.at[q],
            device_id=dev(g, m_pair), device_id_type=MESH,
        )
        copy.start()
        to_pair.append(copy)

    def keep(row_y, q, v):
        v = v * v
        stage[row_y, :, pl.ds(q * WIDTH, WIDTH)] = v
        return jnp.sum(v.reshape(ROWS // 8, 8, WIDTH), axis=0)

    turn = 3 - 2 * y
    totals = []
    for q in range(2):
        mine, other = sums(q)
        totals.append(keep(y + core * turn, q, mine) + keep(y + (1 - core) * turn, q, other))
    for q in range(2):
        to_pair[q].wait()
        totals[q] += keep(pair_y, q, fin[q, 0]) + keep(3 - pair_y, q, fin[q, 1])
    total = jnp.concatenate(totals, axis=1)
    sq[...] = total

    def square_copy(d):
        return pltpu.make_async_remote_copy(
            src_ref=sq, dst_ref=sq_all.at[d - 1], send_sem=qsend.at[d - 1], recv_sem=qrecv.at[d - 1],
            device_id=dev((g + d) % GN, m), device_id_type=MESH,
        )

    for d in range(1, GN):
        square_copy(d).start()
    for d in range(1, GN):
        square_copy(d).wait_recv()
        total += sq_all[d - 1]
    means = jnp.sum(total, axis=0, keepdims=True) / WROWS
    for row_y in range(YN):
        out[pl.ds(row_y * ROWS, ROWS), :] = stage[row_y] / means

    for copy in started:
        copy.wait_send()
    for copy in tile_copies:
        copy.wait_send()
    for s in range(8):
        xt, ct, hop = place(s)
        for c in range(4):
            sibling(s * 4 + c).wait_send()

        @pl.when((hop != 3) | (ct != core))
        def _():
            for c in range(4):
                to_next(s * 4 + c).wait_send()

    for d in range(1, GN):
        square_copy(d).wait_send()


def per_device(slab, tiles, slot_rows):
    dma = pltpu.SemaphoreType.DMA
    return pl.pallas_call(
        body,
        out_shape=jax.ShapeDtypeStruct((256, TILE), F32),
        in_specs=[
            pl.BlockSpec(memory_space=pltpu.HBM),
            pl.BlockSpec(memory_space=pltpu.HBM),
            pl.BlockSpec(memory_space=pltpu.SMEM),
        ],
        out_specs=pl.BlockSpec(memory_space=pltpu.VMEM),
        scratch_shapes=[
            pltpu.VMEM((2, 8, ROWS, KCOLS), F32),
            pltpu.VMEM((2, 2 * TILE, TILE), F32),
            pltpu.VMEM((8, TILE, WIDTH), BF16),
            pltpu.VMEM((8, TILE, WIDTH), BF16),
            pltpu.VMEM((32, 2 * ROWS, TILE), BF16),
            pltpu.VMEM((32, 2 * ROWS, TILE), BF16),
            pltpu.VMEM((32, 2, ROWS, WIDTH), F32),
            pltpu.VMEM((32, ROWS, WIDTH), F32),
            pltpu.VMEM((32, ROWS, WIDTH), F32),
            pltpu.VMEM((32, ROWS, WIDTH), F32),
            pltpu.VMEM((4, 2, ROWS, WIDTH), F32),
            pltpu.VMEM((4, ROWS, WIDTH), F32),
            pltpu.VMEM((2, 2, ROWS, WIDTH), F32),
            pltpu.VMEM((2, 2, ROWS, WIDTH), F32),
            pltpu.VMEM((4, ROWS, TILE), F32),
            pltpu.VMEM((8, TILE), F32),
            pltpu.VMEM((GN - 1, 8, TILE), F32),
            dma((2,)),
            dma((32,)),
            dma((2, 8, 2)),
            dma((2,)),
            dma((2,)),
            dma((32,)),
            dma((32,)),
            dma((32,)),
            dma((32,)),
            dma((4, 2)),
            dma((4,)),
            dma((2,)),
            dma((2,)),
            dma((GN - 1,)),
            dma((GN - 1,)),
        ],
        compiler_params=pltpu.CompilerParams(
            collective_id=0, has_side_effects=True, vmem_limit_bytes=60 * 1024 * 1024
        ),
        name="expand",
    )(slab, tiles, slot_rows)


def solution(mesh):
    return jax.shard_map(
        per_device,
        mesh=mesh,
        in_specs=(P("mem", "grp"), P("grp", "mem"), P("grp", None)),
        out_specs=P("grp", "mem"),
        check_vma=False,
    )
```

time: 111 us -> 123 us (1.11)
  Pallas kernels: 109 us -> 120 us
    pallas_call x1, Pallas kernels: 109 us -> 120 us  [per_device(): pl.pallas_call(body, out_shape=jax.ShapeDtypeStruct((256, TILE), F32), in...]
where the time goes in v2:
time: 123 us; the launch traced here: 122 us
  Pallas kernels  120 us (98%)
  local copies, waits for them, and re-layouts  1.87 us (2%)
    pallas_call x1, Pallas kernels, per_device(): pl.pallas_call(body, out_shape=jax.ShapeDtypeStruct((256, TILE), F32), in...  120 us

profile of v2, /device:TPU:1, one launch (start us, length us, event | category | flops | bytes accessed | tf_op | source)
XLA Modules:
  0.0 122.3 jit_solution(15468774372304618037)
XLA Ops:
  0.0 120.4 %expand.1 = f32[256,512]{1,0:T(8,128)} custom-call(f32[64,2048]{1,0:T(8,128)} %slab.1, f32[1024,512]{1,0:T(8,128)} %tiles.1, s32[2,32]{1,0:T(2,128)} %slot_rows.1), custom_call_target="tpu_custom_call" | custom-call | tf_op jit(solution)/shard_map/expand/pallas_call | solution.py:402
  120.4 1.9 %copy.5 = f32[256,512]{1,0:T(8,128)} copy(f32[256,512]{1,0:T(8,128)} %expand.1) | data formatting | bytes 1048576

commit v3 on v2

--- a/solution.py
+++ b/solution.py
@@ -26,7 +26,7 @@
 
 def body(
     slab, tiles, slot_rows, out,
-    rows, tile_buf, thi, tlo, xhi, xlo, part, sib, csum, mid, dst, near, ybuf, fin, stage, sq, sq_all,
+    rows, tile_buf, thi, tlo, xs, part, sib, csum, mid, dst, near, ybuf, fin, stage, sq, sq_all,
     load_sem, gsend, grecv, tsend, trecv, dsend, drecv, xsend, mrecv, rrecv, nrecv, ysend, yrecv, qsend, qrecv,
 ):
     g = lax.axis_index("grp")
@@ -49,11 +49,12 @@
     load_tiles.start()
 
     barrier = pltpu.get_barrier_semaphore()
-    for mi in (m_up, m_down, m_across, m_pair):
-        pl.semaphore_signal(barrier, inc=1, device_id=dev(g, mi), device_id_type=MESH)
-    for d in range(1, GN):
-        pl.semaphore_signal(barrier, inc=1, device_id=dev((g + d) % GN, m), device_id_type=MESH)
-    pl.semaphore_wait(barrier, 4 + GN - 1)
+    partners = [(g, mi) for mi in (m_up, m_down, m_across, m_pair)] + [(g_sib, m)]
+    for xi in ((x + 1) % XN, (x + XN - 1) % XN):
+        partners += [(xi * 2, m), (xi * 2 + 1, m)]
+    for gi, mi in partners:
+        pl.semaphore_signal(barrier, inc=1, device_id=dev(gi, mi), device_id_type=MESH)
+    pl.semaphore_wait(barrier, len(partners))
 
     started = []
 
@@ -80,8 +81,8 @@
             block = s * 4 + h * 2 + b
             v = rows[w, s, :, pl.ds(h * HALF + b * TILE, TILE)]
             top = v.astype(BF16)
-            xhi[block, pl.ds(w * ROWS, ROWS), :] = top
-            xlo[block, pl.ds(w * ROWS, ROWS), :] = (v - top.astype(F32)).astype(BF16)
+            xs[w, block, pl.ds(0, ROWS), :] = top
+            xs[w, block, pl.ds(ROWS, ROWS), :] = (v - top.astype(F32)).astype(BF16)
 
     def arrive(w, s, h):
         pltpu.make_async_remote_copy(
@@ -106,32 +107,43 @@
                 r = pl.multiple_of(i * 64, 64)
                 v = tile_buf[p, pl.ds(h * TILE + r, 64), pl.ds(q * WIDTH, WIDTH)]
                 top = v.astype(BF16)
-                thi[c * 2 + h, pl.ds(r, 64), :] = top
-                tlo[c * 2 + h, pl.ds(r, 64), :] = (v - top.astype(F32)).astype(BF16)
+                thi[p * 2 + h, pl.ds(r, 64), pl.ds(q * WIDTH, WIDTH)] = top
+                tlo[p * 2 + h, pl.ds(r, 64), pl.ds(q * WIDTH, WIDTH)] = (v - top.astype(F32)).astype(BF16)
                 return carry
             lax.fori_loop(0, TILE // 64, step, 0)
 
-    def product(s, columns):
-        for c in columns:
-            member = m if c < 2 else m_pair
-            u = s * 4 + c
-            total = None
-            for h in range(2):
-                block = s * 4 + jnp.maximum(slot_rows[h, member], 0)
-                a, b = xhi[block], xlo[block]
-                top, low = thi[c * 2 + h], tlo[c * 2 + h]
-                term = (
-                    jnp.dot(a, low, preferred_element_type=F32)
-                    + jnp.dot(b, top, preferred_element_type=F32)
-                    + jnp.dot(a, top, preferred_element_type=F32)
-                )
-                total = term if total is None else total + term
-            part[u] = total.reshape(2, ROWS, WIDTH)
-            sibling(u).start()
-
-    def sibling(u):
+    waiting = [[], [], []]
+
+    def product(items, columns):
+        member = m if columns[0] < 2 else m_pair
+        p = columns[0] // 2
+        lanes = pl.ds(columns[0] % 2 * WIDTH, len(columns) * WIDTH)
+        sums_of = [None] * len(items)
+        for h in range(2):
+            block = jnp.maximum(slot_rows[h, member], 0)
+            pieces = [xs[w, s * 4 + block] for w, s in items]
+            both = jnp.concatenate(pieces, axis=0)
+            tops = jnp.concatenate([v[:ROWS] for v in pieces], axis=0)
+            wide = jnp.dot(both, thi[p * 2 + h, :, lanes], preferred_element_type=F32)
+            low = jnp.dot(tops, tlo[p * 2 + h, :, lanes], preferred_element_type=F32)
+            for i in range(len(items)):
+                r = 2 * i * ROWS
+                term = (wide[r + ROWS : r + 2 * ROWS] + low[i * ROWS : (i + 1) * ROWS]) + wide[r : r + ROWS]
+                sums_of[i] = term if sums_of[i] is None else sums_of[i] + term
+        for i, (w, s) in enumerate(items):
+            for n, c in enumerate(columns):
+                part[w, s * 4 + c] = sums_of[i][:, n * WIDTH : (n + 1) * WIDTH]
+
+            @pl.when(core != w)
+            def _():
+                for c in columns:
+                    sibling(w, s * 4 + c).start()
+
+        waiting[0] += [(w, s, columns) for w, s in items]
+
+    def sibling(w, u):
         return pltpu.make_async_remote_copy(
-            src_ref=part.at[u, 1 - core], dst_ref=sib.at[u],
+            src_ref=part.at[w, u], dst_ref=sib.at[u],
             send_sem=dsend.at[u], recv_sem=drecv.at[u],
             device_id=dev(g_sib, m), device_id_type=MESH,
         )
@@ -166,38 +178,47 @@
             device_id=dev(g_sib, m), device_id_type=MESH,
         )
 
-    def chip_sum(s, columns):
+    def chip_sum(w, s, columns):
         xt, ct, hop = place(s)
-        for c in columns:
-            u = s * 4 + c
-            sibling(u).wait_recv()
-            csum[u] = part[u, core] + sib[u]
-
-            @pl.when(hop == 0)
-            def _():
-                to_next(u).start()
-
-            @pl.when((hop == 3) & (ct != core))
-            def _():
-                to_sibling(u, c).start()
-
-    def chain(s, columns):
+
+        @pl.when(core == w)
+        def _():
+            for c in columns:
+                u = s * 4 + c
+                sibling(w, u).wait_recv()
+                csum[u] = part[w, u] + sib[u]
+
+                @pl.when(hop == 0)
+                def _():
+                    to_next(u).start()
+
+                @pl.when((hop == 3) & (ct != core))
+                def _():
+                    to_sibling(u, c).start()
+
+    def chain(step, w, s, columns):
         xt, ct, hop = place(s)
 
-        @pl.when((hop == 1) | (hop == 2))
+        @pl.when((core == w) & (hop == step))
         def _():
             for c in columns:
                 u = s * 4 + c
                 to_next(u).wait_recv()
                 csum[u] = csum[u] + mid[u]
-
-                @pl.when(hop == 1)
-                def _():
+                if step == 1:
                     to_next(u).start()
-
-                @pl.when(hop == 2)
-                def _():
+                else:
                     to_end(u, c, ct).start()
+
+    def advance():
+        ready, once, twice = waiting
+        for job in twice:
+            chain(2, *job)
+        for job in once:
+            chain(1, *job)
+        for job in ready:
+            chip_sum(*job)
+        waiting[:] = [[], ready, once]
 
     load_slab.wait()
     for h in (LO, HI):
@@ -218,7 +239,10 @@
         arrive(NA, s_down, h)
         move(DOWN, NA, s_down, h)
 
-    first, third, every = (0, 1), (0, 1, 2), (2, 3, 0, 1)
+    own, third, fourth, others = (0, 1), (2,), (3,), (2, 3)
+    near0, near17, near26, near35, far17 = (
+        [(NA, 0), (NB, 0)], [(NA, 1), (NA, 7)], [(NA, 2), (NA, 6)], [(NA, 3), (NA, 5)], [(NB, 1), (NB, 7)]
+    )
     for h in (LO, HI):
         arrive_near(h, 1, 7)
         move(ACROSS, NA, 1, h)
@@ -227,100 +251,104 @@
         split(NA, 7, h)
         arrive(NB, 0, h)
         split(NB, 0, h)
-    product(0, first)
+    product(near0, own)
+    product(near17, own)
     arrive_near(LO, 2, 6)
     arrive(NB, 1, LO)
     move(UP, NB, 1, LO)
     split(NA, 2, LO)
     split(NA, 6, LO)
     split(NB, 1, LO)
-    chip_sum(0, first)
-    arrive_near(HI, 2, 6)
+    advance()
+    arrive(NA, 2, HI)
+    move(UP, NA, 2, HI)
     move(ACROSS, NA, 2, HI)
     arrive(NB, 7, LO)
     move(DOWN, NB, 7, LO)
+    arrive(NA, 6, HI)
+    move(DOWN, NA, 6, HI)
     split(NA, 2, HI)
     split(NA, 6, HI)
     split(NB, 7, LO)
-    chain(0, first)
+    advance()
+    product(near26, own)
     tile_copies[0].wait_recv()
     split_tile(2)
-    product(0, (2,))
+    for items in (near0, near17, near26):
+        product(items, third)
     arrive(NA, 3, LO)
     arrive(NA, 5, LO)
+    advance()
     split(NA, 3, LO)
     split(NA, 5, LO)
     arrive(NB, 1, HI)
     split(NB, 1, HI)
-    product(1, third)
-    chip_sum(0, (2,))
     arrive(NB, 2, LO)
     move(UP, NB, 2, LO)
     move(UP, NA, 3, LO)
     arrive(NB, 6, LO)
     move(DOWN, NB, 6, LO)
+    advance()
     split(NB, 2, LO)
     split(NB, 6, LO)
     arrive(NB, 7, HI)
     split(NB, 7, HI)
-    product(7, third)
-    chip_sum(1, third)
-    chain(0, (2,))
+    product(far17, own)
+    product(far17, third)
     arrive(NA, 3, HI)
     arrive(NA, 5, HI)
     move(ACROSS, NA, 5, HI)
     move(DOWN, NA, 5, HI)
     move(ACROSS, NA, 3, HI)
     move(ACROSS, NA, 6, HI)
+    advance()
     split(NA, 3, HI)
     split(NA, 5, HI)
+    product(near35, own)
+    product(near35, third)
     arrive(NB, 2, HI)
     split(NB, 2, HI)
-    product(2, third)
-    chip_sum(7, third)
-    chain(1, third)
     arrive(NB, 3, LO)
     move(UP, NB, 3, LO)
+    advance()
     arrive(NB, 5, LO)
     split(NB, 3, LO)
     split(NB, 5, LO)
     tile_copies[1].wait_recv()
     split_tile(3)
+    for items in (near0, near17, near26):
+        product(items, fourth)
     arrive(NB, 5, HI)
     move(DOWN, NB, 5, HI)
+    advance()
     split(NB, 5, HI)
-    for s in (0, 1, 7, 2):
-        product(s, (3,))
-    chip_sum(2, third)
-    chain(7, third)
-    product(5, every)
-    for s in (0, 1, 7, 2):
-        chip_sum(s, (3,))
-    chain(2, third)
+    for items in (far17, near35):
+        product(items, fourth)
+    product([(NB, 2), (NB, 5)], others)
+    product([(NB, 2), (NB, 5)], own)
     arrive(NA, 4, LO)
     arrive(NA, 4, HI)
     split(NA, 4, LO)
     split(NA, 4, HI)
     arrive(NB, 3, HI)
     split(NB, 3, HI)
-    product(3, every)
-    chip_sum(5, every)
-    for s in (0, 1, 7, 2):
-        chain(s, (3,))
-    chip_sum(3, every)
+    advance()
+    product([(NA, 4), (NB, 3)], others)
+    product([(NA, 4), (NB, 3)], own)
+    advance()
     for h in (LO, HI):
         arrive(NB, 4, h)
         split(NB, 4, h)
-    product(4, every)
-    chain(5, every)
+    product([(NB, 4)], others)
+    product([(NB, 4)], own)
+    advance()
     arrive(NB, 6, HI)
     split(NB, 6, HI)
-    product(6, every)
-    chip_sum(4, every)
-    chip_sum(6, every)
-    chain(3, every)
-    chain(4, every)
-    chain(6, every)
+    product([(NB, 6)], others)
+    product([(NB, 6)], own)
+    advance()
+    advance()
+    advance()
 
     s_mine = (z - g + ZN) % ZN
 
@@ -337,6 +365,20 @@
         return dst[c, core] + csum[s_mine * 4 + c], dst[c, 1 - core] + near[c]
 
     to_pair = []
+
+    def squares(a, b):
+        return jnp.sum(a * a, axis=0, keepdims=True) + jnp.sum(b * b, axis=0, keepdims=True)
+
+    def square_copy(n):
+        if n < GN - 1:
+            src, target = sq.at[0], dev((g + n + 1) % GN, m)
+        else:
+            src, target = sq.at[1], dev((g + n + 1) % GN, m_pair)
+        return pltpu.make_async_remote_copy(
+            src_ref=src, dst_ref=sq_all.at[n], send_sem=qsend.at[n], recv_sem=qrecv.at[n],
+            device_id=target, device_id_type=MESH,
+        )
+
     for q in range(2):
         mine, other = sums(2 + q)
         ybuf[q, core] = mine
@@ -347,38 +389,21 @@
         )
         copy.start()
         to_pair.append(copy)
-
-    def keep(row_y, q, v):
-        v = v * v
-        stage[row_y, :, pl.ds(q * WIDTH, WIDTH)] = v
-        return jnp.sum(v.reshape(ROWS // 8, 8, WIDTH), axis=0)
+        sq[1, :, pl.ds(q * WIDTH, WIDTH)] = squares(mine, other)
+    for n in range(GN - 1, 2 * GN - 1):
+        square_copy(n).start()
 
     turn = 3 - 2 * y
     totals = []
     for q in range(2):
         mine, other = sums(q)
-        totals.append(keep(y + core * turn, q, mine) + keep(y + (1 - core) * turn, q, other))
-    for q in range(2):
-        to_pair[q].wait()
-        totals[q] += keep(pair_y, q, fin[q, 0]) + keep(3 - pair_y, q, fin[q, 1])
+        stage[y + core * turn, :, pl.ds(q * WIDTH, WIDTH)] = mine * mine
+        stage[y + (1 - core) * turn, :, pl.ds(q * WIDTH, WIDTH)] = other * other
+        totals.append(squares(mine, other))
     total = jnp.concatenate(totals, axis=1)
-    sq[...] = total
-
-    def square_copy(d):
-        return pltpu.make_async_remote_copy(
-            src_ref=sq, dst_ref=sq_all.at[d - 1], send_sem=qsend.at[d - 1], recv_sem=qrecv.at[d - 1],
-            device_id=dev((g + d) % GN, m), device_id_type=MESH,
-        )
-
-    for d in range(1, GN):
-        square_copy(d).start()
-    for d in range(1, GN):
-        square_copy(d).wait_recv()
-        total += sq_all[d - 1]
-    means = jnp.sum(total, axis=0, keepdims=True) / WROWS
-    for row_y in range(YN):
-        out[pl.ds(row_y * ROWS, ROWS), :] = stage[row_y] / means
-
+    sq[0] = total
+    for n in range(GN - 1):
+        square_copy(n).start()
     for copy in started:
         copy.wait_send()
     for copy in tile_copies:
@@ -386,15 +411,26 @@
     for s in range(8):
         xt, ct, hop = place(s)
         for c in range(4):
-            sibling(s * 4 + c).wait_send()
+            sibling(0, s * 4 + c).wait_send()
 
         @pl.when((hop != 3) | (ct != core))
         def _():
             for c in range(4):
                 to_next(s * 4 + c).wait_send()
 
-    for d in range(1, GN):
-        square_copy(d).wait_send()
+    for n in range(2 * GN - 1):
+        square_copy(n).wait_recv()
+        total += sq_all[n]
+    means = total / WROWS
+    for q in range(2):
+        to_pair[q].wait()
+        for w, row_y in enumerate((pair_y, 3 - pair_y)):
+            v = fin[q, w]
+            stage[row_y, :, pl.ds(q * WIDTH, WIDTH)] = v * v
+    for row_y in range(YN):
+        out[pl.ds(row_y * ROWS, ROWS), :] = stage[row_y] / means
+    for n in range(2 * GN - 1):
+        square_copy(n).wait_send()
 
 
 def per_device(slab, tiles, slot_rows):
@@ -411,11 +447,10 @@
         scratch_shapes=[
             pltpu.VMEM((2, 8, ROWS, KCOLS), F32),
             pltpu.VMEM((2, 2 * TILE, TILE), F32),
-            pltpu.VMEM((8, TILE, WIDTH), BF16),
-            pltpu.VMEM((8, TILE, WIDTH), BF16),
-            pltpu.VMEM((32, 2 * ROWS, TILE), BF16),
-            pltpu.VMEM((32, 2 * ROWS, TILE), BF16),
-            pltpu.VMEM((32, 2, ROWS, WIDTH), F32),
+            pltpu.VMEM((4, TILE, TILE), BF16),
+            pltpu.VMEM((4, TILE, TILE), BF16),
+            pltpu.VMEM((2, 32, 2 * ROWS, TILE), BF16),
+            pltpu.VMEM((2, 32, ROWS, WIDTH), F32),
             pltpu.VMEM((32, ROWS, WIDTH), F32),
             pltpu.VMEM((32, ROWS, WIDTH), F32),
             pltpu.VMEM((32, ROWS, WIDTH), F32),
@@ -424,8 +459,8 @@
             pltpu.VMEM((2, 2, ROWS, WIDTH), F32),
             pltpu.VMEM((2, 2, ROWS, WIDTH), F32),
             pltpu.VMEM((4, ROWS, TILE), F32),
-            pltpu.VMEM((8, TILE), F32),
-            pltpu.VMEM((GN - 1, 8, TILE), F32),
+            pltpu.VMEM((2, 1, TILE), F32),
+            pltpu.VMEM((2 * GN - 1, 1, TILE), F32),
             dma((2,)),
             dma((32,)),
             dma((2, 8, 2)),
@@ -439,8 +474,8 @@
             dma((4,)),
             dma((2,)),
             dma((2,)),
-            dma((GN - 1,)),
-            dma((GN - 1,)),
+            dma((2 * GN - 1,)),
+            dma((2 * GN - 1,)),
         ],
         compiler_params=pltpu.CompilerParams(
             collective_id=0, has_side_effects=True, vmem_limit_bytes=60 * 1024 * 1024

time: 123 us -> 98.5 us (0.80)
  Pallas kernels: 120 us -> 96.5 us
    pallas_call x1, Pallas kernels: 120 us -> 96.5 us  [per_device(): pl.pallas_call(body, out_shape=jax.ShapeDtypeStruct((256, TILE), F32), in...]
where the time goes in v3:
time: 98.5 us; the launch traced here: 98.3 us
  Pallas kernels  96.5 us (98%)
  local copies, waits for them, and re-layouts  1.87 us (2%)
    pallas_call x1, Pallas kernels, per_device(): pl.pallas_call(body, out_shape=jax.ShapeDtypeStruct((256, TILE), F32), in...  96.5 us

profile of v3, /device:TPU:1, one launch (start us, length us, event | category | flops | bytes accessed | tf_op | source)
XLA Modules:
  0.0 98.3 jit_solution(11477823752109454511)
XLA Ops:
  0.0 96.5 %expand.1 = f32[256,512]{1,0:T(8,128)} custom-call(f32[64,2048]{1,0:T(8,128)} %slab.1, f32[1024,512]{1,0:T(8,128)} %tiles.1, s32[2,32]{1,0:T(2,128)} %slot_rows.1), custom_call_target="tpu_custom_call" | custom-call | tf_op jit(solution)/shard_map/expand/pallas_call | solution.py:438
  96.5 1.9 %copy.5 = f32[256,512]{1,0:T(8,128)} copy(f32[256,512]{1,0:T(8,128)} %expand.1) | data formatting | bytes 1048576

commit v4 on v3

v4 whole, which is shorter than its diff:
```python
import functools

import jax
import jax.numpy as jnp
from jax import lax
from jax.experimental import pallas as pl
from jax.experimental.pallas import tpu as pltpu
from jax.sharding import PartitionSpec as P

MESH = pl.DeviceIdType.MESH
F32 = jnp.float32
BF16 = jnp.bfloat16

TILE = 512
ROWS = 64
KCOLS = 2048
HALF = 1024
WIDTH = 384
UNITS = ((0, 256), (256, 256), (0, 384), (384, 128))
ZN, YN, XN, GN = 8, 4, 4, 8
WROWS = 2048

UP, DOWN, ACROSS = 0, 1, 2
NA, NB = 0, 1
LO, HI = 0, 1


def body(
    slab, tiles, slot_rows, out,
    rows, tile_buf, thi, tlo, xs, part, sib, csum, mid, dst, near, ybuf, fin, stage, sq, sq_all,
    load_sem, gsend, grecv, tsend, trecv, dsend, drecv, xsend, mrecv, rrecv, nrecv, ysend, yrecv, qsend, qrecv, osem,
):
    g = lax.axis_index("grp")
    m = lax.axis_index("mem")
    x, core = g // 2, g % 2
    z, y = m // YN, m % YN
    pair_y = y + 1 - 2 * (y % 2)
    m_up = ((z + 1) % ZN) * YN + y
    m_down = ((z + ZN - 1) % ZN) * YN + y
    m_across = z * YN + (3 - y)
    m_pair = z * YN + pair_y
    g_sib = x * 2 + (1 - core)

    def dev(gi, mi):
        return {"grp": gi, "mem": mi}

    load_slab = pltpu.make_async_copy(slab, rows.at[0], load_sem.at[0])
    load_tiles = pltpu.make_async_copy(tiles, tile_buf.at[0], load_sem.at[1])
    load_slab.start()
    load_tiles.start()

    barrier = pltpu.get_barrier_semaphore()
    partners = [(g, mi) for mi in (m_up, m_down, m_across, m_pair)] + [(g_sib, m)]
    for xi in ((x + 1) % XN, (x + XN - 1) % XN):
        partners += [(xi * 2, m), (xi * 2 + 1, m)]
    for gi, mi in partners:
        pl.semaphore_signal(barrier, inc=1, device_id=dev(gi, mi), device_id_type=MESH)
    pl.semaphore_wait(barrier, len(partners))

    def piece(w, s, h):
        return rows.at[w * 8 + s, :, pl.ds(h * HALF, HALF)]

    def move(way, w, s, h):
        if way == ACROSS:
            target, tw, ts = m_across, NB, s
        elif way == UP:
            target, tw, ts = m_up, w, s + 1
        else:
            target, tw, ts = m_down, w, (s + 7) % 8
        copy = pltpu.make_async_remote_copy(
            src_ref=piece(w, s, h), dst_ref=piece(tw, ts, h),
            send_sem=gsend, recv_sem=grecv.at[tw, ts, h],
            device_id=dev(g, target), device_id_type=MESH,
        )
        copy.start()

    def split(w, s, h):
        for b in range(2):
            block = s * 4 + h * 2 + b
            v = rows[w * 8 + s, :, pl.ds(h * HALF + b * TILE, TILE)]
            top = v.astype(BF16)
            xs[w, block, pl.ds(0, ROWS), :] = top
            xs[w, block, pl.ds(ROWS, ROWS), :] = (v - top.astype(F32)).astype(BF16)

    def arrive(w, s, h):
        pltpu.make_async_remote_copy(
            src_ref=piece(w, s, h), dst_ref=piece(w, s, h),
            send_sem=gsend, recv_sem=grecv.at[w, s, h],
            device_id=dev(g, m_up), device_id_type=MESH,
        ).wait_recv()

    tile_copies = [
        pltpu.make_async_remote_copy(
            src_ref=tile_buf.at[0, :, pl.ds(*UNITS[2 + q])], dst_ref=tile_buf.at[1, :, pl.ds(*UNITS[2 + q])],
            send_sem=tsend, recv_sem=trecv.at[q],
            device_id=dev(g, m_pair), device_id_type=MESH,
        )
        for q in range(2)
    ]

    def split_tile(c):
        p, lanes = c // 2, pl.ds(*UNITS[c])
        for h in range(2):
            def step(i, carry):
                r = pl.multiple_of(i * 64, 64)
                v = tile_buf[p, pl.ds(h * TILE + r, 64), lanes]
                top = v.astype(BF16)
                thi[p * 2 + h, pl.ds(r, 64), lanes] = top
                tlo[p * 2 + h, pl.ds(r, 64), lanes] = (v - top.astype(F32)).astype(BF16)
                return carry
            lax.fori_loop(0, TILE // 64, step, 0)

    waiting = [[], [], []]

    def product(items, columns):
        member = m if columns[0] < 2 else m_pair
        p = columns[0] // 2
        first = UNITS[columns[0]][0]
        lanes = pl.ds(first, sum(UNITS[c][1] for c in columns))
        sums_of = [None] * len(items)
        for h in range(2):
            block = jnp.maximum(slot_rows[h, member], 0)
            pieces = [xs[w, s * 4 + block] for w, s in items]
            both = jnp.concatenate(pieces, axis=0)
            tops = jnp.concatenate([v[:ROWS] for v in pieces], axis=0)
            wide = jnp.dot(both, thi[p * 2 + h, :, lanes], preferred_element_type=F32)
            low = jnp.dot(tops, tlo[p * 2 + h, :, lanes], preferred_element_type=F32)
            for i in range(len(items)):
                r = 2 * i * ROWS
                term = (wide[r + ROWS : r + 2 * ROWS] + low[i * ROWS : (i + 1) * ROWS]) + wide[r : r + ROWS]
                sums_of[i] = term if sums_of[i] is None else sums_of[i] + term
        for i, (w, s) in enumerate(items):
            for c in columns:
                start, wide = UNITS[c]
                part[w, s * 4 + c, :, pl.ds(0, wide)] = sums_of[i][:, start - first : start - first + wide]

            for owner in range(2):
                theirs = [c for c in columns if (c + w) % 2 == owner]
                if theirs:
                    @pl.when(core != owner)
                    def _():
                        for c in theirs:
                            sibling(w, s, c).start()

        waiting[0] += [(w, s, columns) for w, s in items]

    def unit(w, s, c):
        return (w * 8 + s) * 2 + c // 2

    def cut(c):
        return pl.ds(0, UNITS[c][1])

    def sibling(w, s, c):
        u = unit(w, s, c)
        return pltpu.make_async_remote_copy(
            src_ref=part.at[w, s * 4 + c, :, cut(c)], dst_ref=sib.at[u, :, cut(c)],
            send_sem=dsend, recv_sem=drecv.at[u],
            device_id=dev(g_sib, m), device_id_type=MESH,
        )

    def place(s):
        zt = (z - s + ZN) % ZN
        xt, ct = zt // 2, zt % 2
        dx = (xt - x + XN) % XN
        hop = jnp.where(core == 0, 3 - dx, (dx + 3) % 4)
        return xt, ct, hop

    x_next = (x + 1 + 2 * core) % XN

    def to_next(u, c):
        return pltpu.make_async_remote_copy(
            src_ref=csum.at[u, :, cut(c)], dst_ref=mid.at[u, :, cut(c)],
            send_sem=xsend, recv_sem=mrecv.at[u],
            device_id=dev(x_next * 2 + core, m), device_id_type=MESH,
        )

    def to_end(u, w, c, ct):
        return pltpu.make_async_remote_copy(
            src_ref=csum.at[u, :, cut(c)], dst_ref=dst.at[c, w, :, cut(c)],
            send_sem=xsend, recv_sem=rrecv.at[c, w],
            device_id=dev(x_next * 2 + ct, m), device_id_type=MESH,
        )

    def to_sibling(u, w, c):
        return pltpu.make_async_remote_copy(
            src_ref=csum.at[u, :, cut(c)], dst_ref=near.at[c, w, :, cut(c)],
            send_sem=xsend, recv_sem=nrecv.at[c, w],
            device_id=dev(g_sib, m), device_id_type=MESH,
        )

    def chip_sum(w, s, columns):
        xt, ct, hop = place(s)
        for owner in range(2):
            mine = [c for c in columns if (c + w) % 2 == owner]
            if not mine:
                continue

            @pl.when(core == owner)
            def _():
                for c in mine:
                    u = unit(w, s, c)
                    sibling(w, s, c).wait_recv()
                    csum[u, :, cut(c)] = part[w, s * 4 + c, :, cut(c)] + sib[u, :, cut(c)]

                    @pl.when(hop == 0)
                    def _():
                        to_next(u, c).start()

                    @pl.when((hop == 3) & (ct != core))
                    def _():
                        to_sibling(u, w, c).start()

    def chain(step, w, s, columns):
        xt, ct, hop = place(s)
        for owner in range(2):
            mine = [c for c in columns if (c + w) % 2 == owner]
            if not mine:
                continue

            @pl.when((core == owner) & (hop == step))
            def _():
                for c in mine:
                    u = unit(w, s, c)
                    to_next(u, c).wait_recv()
                    csum[u, :, cut(c)] = csum[u, :, cut(c)] + mid[u, :, cut(c)]
                    if step == 1:
                        to_next(u, c).start()
                    else:
                        to_end(u, w, c, ct).start()

    def advance():
        ready, once, twice = waiting
        for job in twice:
            chain(2, *job)
        for job in once:
            chain(1, *job)
        for job in ready:
            chip_sum(*job)
        waiting[:] = [[], ready, once]

    load_slab.wait()
    for h in (LO, HI):
        move(UP, NA, 0, h)
        move(DOWN, NA, 0, h)
        move(ACROSS, NA, 0, h)
    load_tiles.wait()
    for copy in tile_copies:
        copy.start()
    for h in (LO, HI):
        split(NA, 0, h)
    for c in range(2):
        split_tile(c)

    def arrive_near(h, s_up, s_down):
        arrive(NA, s_up, h)
        move(UP, NA, s_up, h)
        arrive(NA, s_down, h)
        move(DOWN, NA, s_down, h)

    own, third, fourth, others = (0, 1), (2,), (3,), (2, 3)
    near0, near17, near26, near35, far17 = (
        [(NA, 0), (NB, 0)], [(NA, 1), (NA, 7)], [(NA, 2), (NA, 6)], [(NA, 3), (NA, 5)], [(NB, 1), (NB, 7)]
    )
    for h in (LO, HI):
        arrive_near(h, 1, 7)
        move(ACROSS, NA, 1, h)
        move(ACROSS, NA, 7, h)
        split(NA, 1, h)
        split(NA, 7, h)
        arrive(NB, 0, h)
        split(NB, 0, h)
    product(near0, own)
    product(near17, own)
    arrive_near(LO, 2, 6)
    arrive(NB, 1, LO)
    move(UP, NB, 1, LO)
    split(NA, 2, LO)
    split(NA, 6, LO)
    split(NB, 1, LO)
    advance()
    arrive(NA, 2, HI)
    move(UP, NA, 2, HI)
    move(ACROSS, NA, 2, HI)
    arrive(NB, 7, LO)
    move(DOWN, NB, 7, LO)
    arrive(NA, 6, HI)
    move(DOWN, NA, 6, HI)
    split(NA, 2, HI)
    split(NA, 6, HI)
    split(NB, 7, LO)
    advance()
    product(near26, own)
    arrive(NA, 3, LO)
    arrive(NA, 5, LO)
    advance()
    split(NA, 3, LO)
    split(NA, 5, LO)
    arrive(NB, 1, HI)
    split(NB, 1, HI)
    arrive(NB, 2, LO)
    move(UP, NB, 2, LO)
    move(UP, NA, 3, LO)
    arrive(NB, 6, LO)
    move(DOWN, NB, 6, LO)
    advance()
    split(NB, 2, LO)
    split(NB, 6, LO)
    arrive(NB, 7, HI)
    split(NB, 7, HI)
    product(far17, own)
    tile_copies[0].wait_recv()
    split_tile(2)
    for items in (near0, near17, near26, far17):
        product(items, third)
    arrive(NA, 3, HI)
    arrive(NA, 5, HI)
    move(ACROSS, NA, 5, HI)
    move(DOWN, NA, 5, HI)
    move(ACROSS, NA, 3, HI)
    move(ACROSS, NA, 6, HI)
    advance()
    split(NA, 3, HI)
    split(NA, 5, HI)
    product(near35, own)
    product(near35, third)
    arrive(NB, 2, HI)
    split(NB, 2, HI)
    arrive(NB, 3, LO)
    move(UP, NB, 3, LO)
    advance()
    arrive(NB, 5, LO)
    split(NB, 3, LO)
    split(NB, 5, LO)
    tile_copies[1].wait_recv()
    split_tile(3)
    for items in (near0, near17, near26):
        product(items, fourth)
    arrive(NB, 5, HI)
    move(DOWN, NB, 5, HI)
    advance()
    split(NB, 5, HI)
    for items in (far17, near35):
        product(items, fourth)
    product([(NB, 2), (NB, 5)], others)
    product([(NB, 2), (NB, 5)], own)
    arrive(NA, 4, LO)
    arrive(NA, 4, HI)
    split(NA, 4, LO)
    split(NA, 4, HI)
    arrive(NB, 3, HI)
    split(NB, 3, HI)
    product([(NA, 4), (NB, 3)], others)
    product([(NA, 4), (NB, 3)], own)
    advance()
    for h in (LO, HI):
        arrive(NB, 4, h)
        split(NB, 4, h)
    product([(NB, 4)], others)
    product([(NB, 4)], own)
    advance()
    arrive(NB, 6, HI)
    split(NB, 6, HI)
    product([(NB, 6)], others)
    product([(NB, 6)], own)
    advance()
    advance()
    advance()

    s_mine = (z - g + ZN) % ZN

    def received(c, src, sem):
        pltpu.make_async_remote_copy(
            src_ref=csum.at[0, :, cut(c)], dst_ref=src, send_sem=xsend, recv_sem=sem,
            device_id=dev(g_sib, m), device_id_type=MESH,
        ).wait_recv()

    def sums(c):
        rows_of = []
        for w in range(2):
            received(c, dst.at[c, w, :, cut(c)], rrecv.at[c, w])

            @pl.when(core == (c + w) % 2)
            def _():
                near[c, w, :, cut(c)] = csum[unit(w, s_mine, c), :, cut(c)]

            @pl.when(core != (c + w) % 2)
            def _():
                received(c, near.at[c, w, :, cut(c)], nrecv.at[c, w])

            rows_of.append(dst[c, w, :, cut(c)] + near[c, w, :, cut(c)])
        return rows_of

    to_pair = []

    def squares(a, b):
        return jnp.sum(a * a, axis=0, keepdims=True) + jnp.sum(b * b, axis=0, keepdims=True)

    def square_copy(n):
        if n < GN - 1:
            src, target = sq.at[0], dev((g + n + 1) % GN, m)
        else:
            src, target = sq.at[1], dev((g + n + 1) % GN, m_pair)
        return pltpu.make_async_remote_copy(
            src_ref=src, dst_ref=sq_all.at[n], send_sem=qsend, recv_sem=qrecv,
            device_id=target, device_id_type=MESH,
        )

    for q in range(2):
        mine, other = sums(2 + q)
        ybuf[q, 0, :, cut(2 + q)] = mine
        ybuf[q, 1, :, cut(2 + q)] = other
        copy = pltpu.make_async_remote_copy(
            src_ref=ybuf.at[q, :, :, cut(2 + q)], dst_ref=fin.at[q, :, :, cut(2 + q)], send_sem=ysend, recv_sem=yrecv.at[q],
            device_id=dev(g, m_pair), device_id_type=MESH,
        )
        copy.start()
        to_pair.append(copy)
        sq[1, :, pl.ds(*UNITS[2 + q])] = squares(mine, other)
    for n in range(GN - 1, 2 * GN - 1):
        square_copy(n).start()

    totals = []
    for q in range(2):
        mine, other = sums(q)
        stage[y, :, pl.ds(*UNITS[q])] = mine * mine
        stage[3 - y, :, pl.ds(*UNITS[q])] = other * other
        totals.append(squares(mine, other))
    total = jnp.concatenate(totals, axis=1)
    sq[0] = total
    for n in range(GN - 1):
        square_copy(n).start()
    def all_sent(sem, ref):
        pltpu.make_async_remote_copy(
            src_ref=ref, dst_ref=ref, send_sem=sem, recv_sem=sem,
            device_id=dev(g_sib, m), device_id_type=MESH,
        ).wait_send()

    all_sent(gsend, rows.at[pl.ds(0, 15)])
    all_sent(tsend, tile_buf.at[0])
    all_sent(dsend, rows.at[pl.ds(0, 4)])
    all_sent(xsend, rows.at[pl.ds(0, 7), :, pl.ds(0, HALF)])
    all_sent(ysend, stage.at[pl.ds(0, 2)])

    pltpu.make_async_remote_copy(
        src_ref=sq_all, dst_ref=sq_all, send_sem=qsend, recv_sem=qrecv,
        device_id=dev(g_sib, m), device_id_type=MESH,
    ).wait()
    for n in range(2 * GN - 1):
        total += sq_all[n]
    means = total / WROWS
    for q in range(2):
        to_pair[q].wait_recv()
        for w, row_y in enumerate((pair_y, 3 - pair_y)):
            v = fin[q, w, :, cut(2 + q)]
            stage[row_y, :, pl.ds(*UNITS[2 + q])] = v * v
    leaves = []
    for row_y in range(YN):
        stage[row_y] = stage[row_y] / means
        leave = pltpu.make_async_copy(stage.at[row_y], out.at[pl.ds(row_y * ROWS, ROWS), :], osem.at[row_y])
        leave.start()
        leaves.append(leave)
    for leave in leaves:
        leave.wait()


def per_device(slab, tiles, slot_rows):
    dma = pltpu.SemaphoreType.DMA
    return pl.pallas_call(
        body,
        out_shape=jax.ShapeDtypeStruct((256, TILE), F32),
        in_specs=[
            pl.BlockSpec(memory_space=pltpu.HBM),
            pl.BlockSpec(memory_space=pltpu.HBM),
            pl.BlockSpec(memory_space=pltpu.SMEM),
        ],
        out_specs=pl.BlockSpec(memory_space=pltpu.HBM),
        scratch_shapes=[
            pltpu.VMEM((16, ROWS, KCOLS), F32),
            pltpu.VMEM((2, 2 * TILE, TILE), F32),
            pltpu.VMEM((4, TILE, TILE), BF16),
            pltpu.VMEM((4, TILE, TILE), BF16),
            pltpu.VMEM((2, 32, 2 * ROWS, TILE), BF16),
            pltpu.VMEM((2, 32, ROWS, WIDTH), F32),
            pltpu.VMEM((32, ROWS, WIDTH), F32),
            pltpu.VMEM((32, ROWS, WIDTH), F32),
            pltpu.VMEM((32, ROWS, WIDTH), F32),
            pltpu.VMEM((4, 2, ROWS, WIDTH), F32),
            pltpu.VMEM((4, 2, ROWS, WIDTH), F32),
            pltpu.VMEM((2, 2, ROWS, WIDTH), F32),
            pltpu.VMEM((2, 2, ROWS, WIDTH), F32),
            pltpu.VMEM((4, ROWS, TILE), F32),
            pltpu.VMEM((2, 1, TILE), F32),
            pltpu.VMEM((2 * GN - 1, 1, TILE), F32),
            dma((2,)),
            dma,
            dma((2, 8, 2)),
            dma,
            dma((2,)),
            dma,
            dma((32,)),
            dma,
            dma((32,)),
            dma((4, 2)),
            dma((4, 2)),
            dma,
            dma((2,)),
            dma,
            dma,
            dma((4,)),
        ],
        compiler_params=pltpu.CompilerParams(
            collective_id=0, has_side_effects=True, vmem_limit_bytes=60 * 1024 * 1024
        ),
        name="expand",
    )(slab, tiles, slot_rows)


def solution(mesh):
    return jax.shard_map(
        per_device,
        mesh=mesh,
        in_specs=(P("mem", "grp"), P("grp", "mem"), P("grp", None)),
        out_specs=P("grp", "mem"),
        check_vma=False,
    )
```

time: 98.5 us -> 95.9 us (0.974)
  Pallas kernels: 96.5 us -> 93.9 us
    pallas_call x1, Pallas kernels: 96.5 us -> 93.9 us  [per_device(): pl.pallas_call(body, out_shape=jax.ShapeDtypeStruct((256, TILE), F32), in...]
where the time goes in v4:
time: 95.9 us; the launch traced here: 95.8 us
  Pallas kernels  93.9 us (98%)
  local copies, waits for them, and re-layouts  1.87 us (2%)
    pallas_call x1, Pallas kernels, per_device(): pl.pallas_call(body, out_shape=jax.ShapeDtypeStruct((256, TILE), F32), in...  93.9 us

profile of v4, /device:TPU:1, one launch (start us, length us, event | category | flops | bytes accessed | tf_op | source)
XLA Modules:
  0.0 95.8 jit_solution(8726107949771495073)
XLA Ops:
  0.0 93.9 %expand.1 = f32[256,512]{1,0:T(8,128)} custom-call(f32[64,2048]{1,0:T(8,128)} %slab.1, f32[1024,512]{1,0:T(8,128)} %tiles.1, s32[2,32]{1,0:T(2,128)} %slot_rows.1), custom_call_target="tpu_custom_call" | custom-call | tf_op jit(solution)/shard_map/expand/pallas_call | solution.py:468
  93.9 1.9 %copy.5 = f32[256,512]{1,0:T(8,128)} copy(f32[256,512]{1,0:T(8,128)} %expand.1) | data formatting | bytes 1048576

commit v5 on v4

--- a/solution.py
+++ b/solution.py
@@ -355,13 +355,10 @@
     for h in (LO, HI):
         arrive(NB, 4, h)
         split(NB, 4, h)
-    product([(NB, 4)], others)
-    product([(NB, 4)], own)
-    advance()
     arrive(NB, 6, HI)
     split(NB, 6, HI)
-    product([(NB, 6)], others)
-    product([(NB, 6)], own)
+    product([(NB, 4), (NB, 6)], others)
+    product([(NB, 4), (NB, 6)], own)
     advance()
     advance()
     advance()

time: 95.9 us -> 93.6 us (0.976)
  Pallas kernels: 93.9 us -> 91.5 us
    pallas_call x1, Pallas kernels: 93.9 us -> 91.5 us  [per_device(): pl.pallas_call(body, out_shape=jax.ShapeDtypeStruct((256, TILE), F32), in...]
where the time goes in v5:
time: 93.6 us; the launch traced here: 93.4 us
  Pallas kernels  91.5 us (98%)
  local copies, waits for them, and re-layouts  1.87 us (2%)
    pallas_call x1, Pallas kernels, per_device(): pl.pallas_call(body, out_shape=jax.ShapeDtypeStruct((256, TILE), F32), in...  91.5 us

profile of v5, /device:TPU:1, one launch (start us, length us, event | category | flops | bytes accessed | tf_op | source)
XLA Modules:
  0.0 93.4 jit_solution(10981943087151978196)
XLA Ops:
  0.0 91.5 %expand.1 = f32[256,512]{1,0:T(8,128)} custom-call(f32[64,2048]{1,0:T(8,128)} %slab.1, f32[1024,512]{1,0:T(8,128)} %tiles.1, s32[2,32]{1,0:T(2,128)} %slot_rows.1), custom_call_target="tpu_custom_call" | custom-call | tf_op jit(solution)/shard_map/expand/pallas_call | solution.py:465
  91.6 1.9 %copy.5 = f32[256,512]{1,0:T(8,128)} copy(f32[256,512]{1,0:T(8,128)} %expand.1) | data formatting | bytes 1048576
